TPU v7x, 256 devices: a whole 4x4x8 slice. The times are simulated.
256 devices in a mesh: dp: 32 (over z, x_lo, core), comp: 8 (over y, x_hi).
Axes of the slice: x: 4 (x_hi: 2, x_lo: 2; x = x_hi * 2 + x_lo), y: 4, z: 8, core: 2. Of those that a mesh axis runs over, the one named last changes fastest.
Arguments:
- points: float32 [262144, 128], P('dp'), may hold values from -8 to 8
- means: float32 [4096, 128], P('comp'), may hold values from -3 to 3
- variances: float32 [4096, 128], P('comp'), may hold values from 0.5 to 4
- log_weights: float32 [4096], P('comp'), may hold values from -2 to 2
Outputs:
- log_lik: float32 [262144], P('dp')
- new_means: float32 [4096, 128], P('comp')
- new_variances: float32 [4096, 128], P('comp')
- new_log_weights: float32 [4096], P('comp')
All inputs are finite; a program needn't handle non-finite values.
Results may differ from a plain program's by a relative error of at most 0.0003.
Values sent between devices are 32-bit elements; how exact they have to be, the bound alone decides.
No kernel may reach another device: no remote copies, remote signals or barrier semaphores. Data moves between devices by JAX's collectives and lax.ppermute only.
A program may use at most 128 MiB of HBM per device.

v0:
```python
import functools
import math

import jax
import jax.numpy as jnp
from jax import lax
from jax.experimental import pallas as pl
from jax.experimental.pallas import tpu as pltpu
from jax.sharding import Mesh, PartitionSpec as P

LOG_TWO_PI = math.log(2.0 * math.pi)
LOG2E = math.log2(math.e)
LN2 = math.log(2.0)
PRIOR = 1.0
LIMIT = 10
FIRST = 1024
TILE = 256
GROUPS = 16
PARTS = 4
F32 = jnp.float32
BF16 = jnp.bfloat16

DP = ("z", "xl", "co")
RING = ("xl", "z")
COMP = ("y", "xh")
ROWS = 16
TALL = 40

NT = (((1,), (1,)), ((), ()))


def halves(a):
    high = a.astype(BF16)
    low = (a - high.astype(F32)).astype(BF16)
    return high, low


def point_halves(x):
    xh, xl = halves(x)
    qh, ql = halves(x * x)
    return jnp.concatenate([xh, qh], axis=1), jnp.concatenate([xl, ql], axis=1)


def density_kernel(table_ref, x_hbm, mean_hbm, var_hbm, logw_hbm, e_ref, p_ref, q_ref, m_ref, l_ref, own_ref, w_ref, v_ref, off_ref, mean_ref, var_ref, logw_ref, x_ref, sems):
    n, d = x_ref.shape
    cuts = (0, FIRST, n)
    copies = [
        pltpu.make_async_copy(mean_hbm, mean_ref, sems.at[0]),
        pltpu.make_async_copy(var_hbm, var_ref, sems.at[1]),
        pltpu.make_async_copy(logw_hbm, logw_ref, sems.at[2]),
    ]
    chunks = [
        pltpu.make_async_copy(
            x_hbm.at[low:high, :], x_ref.at[low:high, :], sems.at[3 + i]
        )
        for i, (low, high) in enumerate(zip(cuts, cuts[1:]))
    ]
    for copy in copies + chunks:
        copy.start()
    for copy in copies:
        copy.wait()
    mean = mean_ref[...]
    var = var_ref[...]
    inverse = 1.0 / var
    scaled = mean * inverse
    size = jnp.sum(mean * scaled + jnp.log(var), axis=1, keepdims=True)
    logw = jnp.swapaxes(jnp.broadcast_to(logw_ref[...], (128, logw_ref.shape[1])), 0, 1)
    off = (logw - 0.5 * (size + d * LOG_TWO_PI)) * LOG2E
    off_ref[...] = jnp.broadcast_to(off[:, :1], off_ref.shape)
    w = jnp.concatenate([scaled * LOG2E, inverse * (-0.5 * LOG2E)], axis=1)
    w_ref[...], v_ref[...] = halves(w)
    begin = pl.multiple_of(table_ref[4], ROWS)
    own_ref[:ROWS, :] = mean_ref[pl.ds(begin, ROWS), :]
    own_ref[ROWS:, :] = var_ref[pl.ds(begin, ROWS), :]
    wh = w_ref[...]
    wl = v_ref[...]
    groups, size = GROUPS, wh.shape[0] // GROUPS

    def mul(a, b):
        return lax.dot_general(a, b, NT, preferred_element_type=F32)

    for tile in range(n // TILE):
        if tile * TILE in cuts:
            chunks[cuts.index(tile * TILE)].wait()
        rows = slice(tile * TILE, (tile + 1) * TILE)
        ph, plo = point_halves(x_ref[rows, :])
        p_ref[rows, :] = ph
        q_ref[rows, :] = plo
        logp = mul(wh, ph) + mul(wl, ph) + mul(wh, plo)
        tops = []
        sums = []
        for g in range(groups):
            at = slice(g * size, (g + 1) * size)
            part = logp[at, :] + off_ref[at, :]
            part = part.reshape(size // 8, 8, TILE)
            top = jnp.max(part, axis=0)
            e = jnp.exp2(part - top[None])
            e_ref[tile, at, :] = e.reshape(size, TILE)
            m_ref[8 * g : 8 * g + 8, rows] = top
            tops.append(top)
            sums.append(jnp.sum(e, axis=0))
        top = jnp.max(functools.reduce(jnp.maximum, tops), axis=0, keepdims=True)
        s = sum(a * jnp.exp2(t - top) for a, t in zip(sums, tops))
        local = top + jnp.log2(jnp.sum(s, axis=0, keepdims=True))
        for j in range(TILE // 128):
            row = tile * (TILE // 128) + j
            part = local[:, j * 128 : (j + 1) * 128]
            l_ref[:, row : row + 1, :] = jnp.broadcast_to(part[None], (l_ref.shape[0], 1, 128))


def densities(points, means, variances, log_weights, table, copies):
    n, d = points.shape
    k = means.shape[0]
    hbm, vmem, smem = (
        pl.BlockSpec(memory_space=s) for s in (pltpu.HBM, pltpu.VMEM, pltpu.SMEM)
    )
    return pl.pallas_call(
        density_kernel,
        in_specs=[smem] + [hbm] * 4,
        out_specs=[vmem] * 6,
        scratch_shapes=[
            pltpu.VMEM((k, 2 * d), BF16),
            pltpu.VMEM((k, 2 * d), BF16),
            pltpu.VMEM((k, TILE), F32),
            pltpu.VMEM((k, d), F32),
            pltpu.VMEM((k, d), F32),
            pltpu.VMEM((1, k), F32),
            pltpu.VMEM((n, d), F32),
            pltpu.SemaphoreType.DMA((5,)),
        ],
        out_shape=[
            pltpu.VMEM((n // TILE, k, TILE), F32),
            pltpu.VMEM((n, 2 * d), BF16),
            pltpu.VMEM((n, 2 * d), BF16),
            pltpu.VMEM((8 * GROUPS, n), F32),
            pltpu.VMEM((copies, n // 128, 128), F32),
            pltpu.VMEM((2 * ROWS, d), F32),
        ],
        compiler_params=pltpu.CompilerParams(vmem_limit_bytes=LIMIT << 20),
        cost_estimate=pl.CostEstimate(
            flops=12 * n * k * d, bytes_accessed=4 * n * (k + d), transcendentals=n * k
        ),
        name="density",
    )(
        table,
        in_hbm(points),
        in_hbm(means),
        in_hbm(variances),
        in_hbm(log_weights.reshape(1, k)),
    )


def in_hbm(array):
    return pltpu.with_memory_space_constraint(array, pltpu.HBM)


def in_vmem(*arrays):
    return [pltpu.with_memory_space_constraint(a, pltpu.VMEM) for a in arrays]


def moment_kernel(table_ref, e_ref, p_ref, q_ref, m_ref, sum_ref, *refs, block, first, places):
    if first:
        lik_hbm, total_ref, *refs = refs
        *refs, lik_ref, sem = refs
    else:
        total_ref = sum_ref
    *out_refs, acc_ref, cnt_ref = refs
    step = pl.program_id(0)
    size = e_ref.shape[1] // GROUPS
    pieces, _, d = out_refs[0].shape
    groups = pieces * ROWS // size

    @pl.when(step == 0)
    def _():
        acc_ref[...] = jnp.zeros_like(acc_ref)
        cnt_ref[...] = jnp.zeros_like(cnt_ref)
        if first:
            sums = sum_ref[...]
            top = jnp.max(sums, axis=0)
            total = top + jnp.log2(jnp.sum(jnp.exp2(sums - top[None]), axis=0))
            total_ref[...] = total
            lik_ref[...] = total * LN2
            pltpu.make_async_copy(lik_ref, lik_hbm, sem).start()

    def mul(a, b):
        return jnp.dot(a, b, preferred_element_type=F32)

    acc = None
    for tile in range(0, block, TILE):
        some = pl.ds(pl.multiple_of(step * block + tile, TILE), TILE)
        index = step * (block // TILE) + tile // TILE
        lanes = TILE // 128
        total = jnp.concatenate(
            [total_ref[pl.ds(index * lanes + j, 1), :] for j in range(lanes)], axis=1
        )
        parts = []
        for place in places:
            for g in range(groups):
                at = table_ref[place] * groups + g
                rows = pl.ds(pl.multiple_of(at * size, size), size)
                part = e_ref[index, rows, :].reshape(size // 8, 8, TILE)
                tops = m_ref[pl.ds(pl.multiple_of(at * 8, 8), 8), some]
                parts.append((part * jnp.exp2(tops - total)[None]).reshape(size, TILE))
        resp = jnp.concatenate(parts, axis=0)
        part = sum(resp[:, i : i + 128] for i in range(0, TILE, 128))
        count = part if tile == 0 else count + part
        rh, rl = halves(resp)
        ph = p_ref[some, :]
        part = mul(rh, ph) + mul(rl, ph) + mul(rh, q_ref[some, :])
        acc = part if tile == 0 else acc + part
    cnt_ref[...] += count
    acc_ref[...] += acc

    @pl.when(step == pl.num_programs(0) - 1)
    def _():
        if first:
            pltpu.make_async_copy(lik_ref, lik_hbm, sem).wait()
        count = jnp.sum(cnt_ref[...], axis=1, keepdims=True)
        count = jnp.broadcast_to(count, cnt_ref.shape).reshape(-1, pieces, 2, ROWS // 2, d)
        lane = lax.broadcasted_iota(jnp.int32, (pieces, ROWS // 2, d), 2)
        for i, out_ref in enumerate(out_refs):
            at = slice(i * pieces * ROWS, (i + 1) * pieces * ROWS)
            out_ref[:, 0:ROWS, :] = acc_ref[at, :d].reshape(pieces, ROWS, d)
            out_ref[:, ROWS : 2 * ROWS, :] = acc_ref[at, d:].reshape(pieces, ROWS, d)
            out_ref[:, 2 * ROWS :, :] = jnp.where(lane < d // 2, count[i, :, 0], count[i, :, 1])


def moments(table, places, e, p, q, m, sums, block, first):
    k = e.shape[1] // PARTS
    n, d = p.shape[0], p.shape[1] // 2
    pieces = k // ROWS
    rows = k * len(places)
    vmem = pl.BlockSpec(memory_space=pltpu.VMEM)

    def kernel(*refs):
        moment_kernel(*refs, block=block, first=first, places=places)

    out_specs = [vmem for _ in places]
    out_shape = [pltpu.VMEM((pieces, TALL, d), F32) for _ in places]
    scratch = [pltpu.VMEM((rows, 2 * d), F32), pltpu.VMEM((rows, 128), F32)]
    if first:
        out_specs = [pl.BlockSpec(memory_space=pltpu.HBM), vmem, *out_specs]
        out_shape = [pltpu.HBM((n // 128, 128), F32), pltpu.VMEM((n // 128, 128), F32), *out_shape]
        scratch += [pltpu.VMEM((n // 128, 128), F32), pltpu.SemaphoreType.DMA]
    return pl.pallas_call(
        kernel,
        grid_spec=pltpu.PrefetchScalarGridSpec(
            num_scalar_prefetch=1,
            grid=(n // block,),
            in_specs=[vmem] * 5,
            out_specs=out_specs,
            scratch_shapes=scratch,
        ),
        out_shape=out_shape,
        compiler_params=pltpu.CompilerParams(vmem_limit_bytes=LIMIT << 20),
        cost_estimate=pl.CostEstimate(
            flops=12 * n * rows * d, bytes_accessed=4 * n * (rows + d), transcendentals=n
        ),
        name="moment",
    )(table, *in_vmem(e, p, q, m, sums))


def summed(*arrays):
    def kernel(*refs):
        refs[-1][...] = functools.reduce(lambda a, b: a + b, [r[...] for r in refs[:-1]])

    return pl.pallas_call(
        kernel,
        out_shape=pltpu.VMEM(arrays[0].shape, F32),
        compiler_params=pltpu.CompilerParams(vmem_limit_bytes=2 << 20),
        name="add",
    )(*in_vmem(*arrays))


def update_kernel(part_ref, own_ref, out_ref, *, points, comps):
    s = jnp.sum(part_ref[...], axis=0)
    d = s.shape[1]
    first = s[:ROWS]
    second = s[ROWS : 2 * ROWS]
    pair = s[2 * ROWS :]
    count = jnp.concatenate([pair[:, :1], pair[:, d // 2 : d // 2 + 1]], axis=0)
    denom = count + PRIOR
    mean = own_ref[:ROWS, :]
    var = own_ref[ROWS:, :]
    fresh = (first + PRIOR * mean) / denom
    fresh_var = (second + PRIOR * (var + mean * mean)) / denom - fresh * fresh
    logw = jnp.log((pair + PRIOR) / (points + PRIOR * comps))
    for i in range(out_ref.shape[0]):
        out_ref[i, :ROWS, :] = fresh
        out_ref[i, ROWS : 2 * ROWS, :] = fresh_var
        out_ref[i, 2 * ROWS :, :] = logw


def unpack_kernel(at_ref, *refs):
    *parts, mean_ref, var_ref, logw_ref = refs
    d = mean_ref.shape[1]
    rows = mean_ref.shape[0] // len(parts)
    for i, ref in enumerate(parts):
        at = pl.ds(pl.multiple_of((at_ref[0] if i == 0 else 1 - at_ref[0]) * rows, rows), rows)
        mean_ref[at, :] = ref[:, :ROWS, :].reshape(rows, d)
        var_ref[at, :] = ref[:, ROWS : 2 * ROWS, :].reshape(rows, d)
        pair = ref[:, 2 * ROWS :, :]
        both = jnp.concatenate(
            [
                jnp.broadcast_to(pair[:, :, :1], pair.shape),
                jnp.broadcast_to(pair[:, :, d // 2 : d // 2 + 1], pair.shape),
            ],
            axis=1,
        ).reshape(rows, d)
        logw_ref[:, at] = jnp.swapaxes(both, 0, 1)[:1, :]


def exchanged(array, axis):
    return lax.ppermute(array, axis, [(0, 1), (1, 0)])


def per_device(points, means, variances, log_weights):
    n, d = points.shape
    k = means.shape[0]
    total_points = float(n * lax.axis_size(DP))
    total_comps = float(k * lax.axis_size(COMP))
    ring = lax.axis_size(RING)
    core = lax.axis_index("co")
    side = lax.axis_index("xl")
    begin = (core * 2 + side) * (k // 4) + lax.axis_index("z") * ROWS
    far = 1 - core
    table = jnp.stack([far * 2 + 1 - side, core * 2 + 1 - side, far * 2 + side, core * 2 + side, begin])
    e, p, q, m, local, own = densities(
        points, means, variances, log_weights, table, lax.axis_size(COMP)
    )
    everyone = lax.all_to_all(local, COMP, 0, 0, tiled=True)

    def some(places, sums, first=False):
        return moments(table, places, e, p, q, m, sums, n, first)

    lik, total, away = some((0,), everyone, True)
    away = exchanged(away, "co")
    (near,) = some((1,), total)
    away, total = lax.optimization_barrier((summed(near, away), total))
    away = exchanged(away, "xl")
    (other,) = some((2,), total)
    other = exchanged(other, "co")
    (mine,) = some((3,), total)
    parts = lax.all_to_all(summed(mine, other, away), "z", 0, 0, tiled=True)

    def update(*refs):
        update_kernel(*refs, points=total_points, comps=total_comps)

    part = pl.pallas_call(
        update, out_shape=pltpu.VMEM((ring, TALL, d), F32), name="update"
    )(*in_vmem(parts, own))
    near = lax.all_to_all(part, RING, 0, 0, tiled=True)
    fresh = [near, exchanged(near, "co")]
    smem, vmem = (pl.BlockSpec(memory_space=s) for s in (pltpu.SMEM, pltpu.VMEM))
    fresh_means, fresh_vars, fresh_logw = pl.pallas_call(
        unpack_kernel,
        in_specs=[smem] + [vmem] * 2,
        out_shape=[
            jax.ShapeDtypeStruct((k, d), F32),
            jax.ShapeDtypeStruct((k, d), F32),
            jax.ShapeDtypeStruct((1, k), F32),
        ],
        name="unpack",
    )(core.reshape(1), *in_vmem(*fresh))
    return (lik.reshape(n), fresh_means, fresh_vars, fresh_logw.reshape(k))


def solution(mesh):
    fine = Mesh(mesh.devices.reshape(8, 2, 2, 4, 2), DP + COMP)
    in_specs = (P(DP, None), P(COMP, None), P(COMP, None), P(COMP))
    out_specs = (P(DP), P(COMP, None), P(COMP, None), P(COMP))
    return jax.shard_map(
        per_device, mesh=fine, in_specs=in_specs, out_specs=out_specs, check_vma=False
    )
```

profile of v0, /device:TPU:1, one launch (start us, length us, event | category | flops | bytes accessed | tf_op | source)
XLA Modules:
  0.0 74.8 jit_solution(1345611551930417737)
XLA Ops:
  0.6 0.1 stack.23.table_ref.refs_0_
  0.7 9.5 %density.1 = (f32[32,512,256]{2,1,0:T(8,128)S(1)}, bf16[8192,256]{1,0:T(8,128)(2,1)S(1)}, bf16[8192,256]{1,0:T(8,128)(2,1)S(1)}, f32[128,8192]{1,0:T(8,128)S(1)}...) custom-call(s32[5]{0:T(128)S(1)} %stack.23.table_ref.refs_0_, f32[8192,128]{1,0:T(8,128)} %x_hbm.1, ...), custom_call_target="tpu_custom_call" | custom-call | flops 6442450944 | bytes 20971520 | tf_op jit(solution)/shard_map/density/pallas_call | solution.py:117
  10.2 14.9 %all_to_all.15.refs_5_ = f32[8,64,128]{2,1,0:T(8,128)S(1)} all-to-all(f32[8,64,128]{2,1,0:T(8,128)S(1)} %get-tuple-element.22), channel_id=1, replica_groups=mesh['z'=8,'xl'=2,'co'=2,'y'=4,'xh'=2] {'y','xh'}, dimensions={0} | all-to-all | bytes 524288 | tf_op jit(solution)/shard_map/all_to_all | solution.py:331
  25.1 3.2 %moment.4 = (f32[64,128]{1,0:T(8,128)}, f32[64,128]{1,0:T(8,128)S(1)}, f32[8,40,128]{2,1,0:T(8,128)S(1)}) custom-call(s32[5]{0:T(128)S(1)} %stack.23.table_ref.refs_0_, f32[32,512,256]{2,1,0:T(8,128)S(1)} %get-tuple-element.18.refs_1_, bf16[8192,256]{1,0:T(8,128)(2,1)S(1)} %get-tuple-element.19.refs_2_, bf16[8192,256]{1,0:T(8,128)(2,1)S(1)} %get-tuple-element.20.refs_3_, ...), custom_call_target="tpu_custom_call" | custom-call | flops 1610612736 | bytes 8388608 | tf_op jit(solution)/shard_map/moment/pallas_call | solution.py:245
  28.3 2.4 %collective-permute-start = (f32[8,40,128]{2,1,0:T(8,128)S(1)}, f32[8,40,128]{2,1,0:T(8,128)S(1)}, u32[]{:S(2)}, u32[]{:S(2)}) collective-permute-start(f32[8,40,128]{2,1,0:T(8,128)S(1)} %get-tuple-element.25), channel_id=1, source_target_pairs={{0,8},{8,0},{1,9},{9,1},{2,10},{10,2},{3,11},{11,3},{4,12},{12,4},... | collective-permute-start | bytes 491528 | tf_op jit(solution)/shard_map/ppermute | solution.py:314
  30.6 2.5 %moment.5.refs_0_ = f32[8,40,128]{2,1,0:T(8,128)S(1)} custom-call(s32[5]{0:T(128)S(1)} %stack.23.table_ref.refs_0_, f32[32,512,256]{2,1,0:T(8,128)S(1)} %get-tuple-element.18.refs_1_, bf16[8192,256]{1,0:T(8,128)(2,1)S(1)} %get-tuple-element.19.refs_2_, bf16[8192,256]{1,0:T(8,128)(2,1)S(1)} %get-tuple-element.20.refs_3_, ...), custom_call_target="tpu_custom_call" | custom-call | flops 1610612736 | bytes 8388608 | tf_op jit(solution)/shard_map/moment/pallas_call | solution.py:245
  33.2 0.0 collective-permute-done.refs_1_
  33.2 2.5 %moment.7 = f32[8,40,128]{2,1,0:T(8,128)S(1)} custom-call(s32[5]{0:T(128)S(1)} %stack.23.table_ref.refs_0_, f32[32,512,256]{2,1,0:T(8,128)S(1)} %get-tuple-element.18.refs_1_, bf16[8192,256]{1,0:T(8,128)(2,1)S(1)} %get-tuple-element.19.refs_2_, bf16[8192,256]{1,0:T(8,128)(2,1)S(1)} %get-tuple-element.20.refs_3_, f32[128,8192]{1,0:T(8,128)S(1)} %get-tuple-element.21.refs_4_, ...), custom_call_target="tpu_custom_call" | custom-call | flops 1610612736 | bytes 8388608 | tf_op jit(solution)/shard_map/moment/pallas_call | solution.py:245
  35.7 0.1 collective-permute-start.1
  35.8 0.4 collective-permute-start.2
  36.2 2.5 %moment.6.refs_0_ = f32[8,40,128]{2,1,0:T(8,128)S(1)} custom-call(s32[5]{0:T(128)S(1)} %stack.23.table_ref.refs_0_, f32[32,512,256]{2,1,0:T(8,128)S(1)} %get-tuple-element.18.refs_1_, bf16[8192,256]{1,0:T(8,128)(2,1)S(1)} %get-tuple-element.19.refs_2_, bf16[8192,256]{1,0:T(8,128)(2,1)S(1)} %get-tuple-element.20.refs_3_, ...), custom_call_target="tpu_custom_call" | custom-call | flops 1610612736 | bytes 8388608 | tf_op jit(solution)/shard_map/moment/pallas_call | solution.py:245
  38.8 0.0 collective-permute-done.1.refs_1_
  38.8 2.5 %collective-permute-done.2.refs_2_ = f32[8,40,128]{2,1,0:T(8,128)S(1)} collective-permute-done((f32[8,40,128]{2,1,0:T(8,128)S(1)}, f32[8,40,128]{2,1,0:T(8,128)S(1)}, u32[]{:S(2)}, u32[]{:S(2)}) %collective-permute-start.2) | collective-permute-done | bytes 163872 | tf_op jit(solution)/shard_map/ppermute | solution.py:314
  41.3 16.4 %all_to_all.16.refs_0_ = f32[8,40,128]{2,1,0:T(8,128)S(1)} all-to-all(f32[8,40,128]{2,1,0:T(8,128)S(1)} %add.24), channel_id=1, replica_groups=mesh['z'=8,'xl'=2,'co'=2,'y'=4,'xh'=2] {'z'}, dimensions={0} | all-to-all | bytes 327680 | tf_op jit(solution)/shard_map/all_to_all | solution.py:344
  57.7 0.2 update.1
  57.8 10.8 %all_to_all.17.refs_0_ = f32[16,40,128]{2,1,0:T(8,128)S(1)} all-to-all(f32[16,40,128]{2,1,0:T(8,128)S(1)} %update.1), channel_id=1, replica_groups=mesh['z'=8,'xl'=2,'co'=2,'y'=4,'xh'=2] {'xl','z'}, dimensions={0} | all-to-all | bytes 655360 | tf_op jit(solution)/shard_map/all_to_all | solution.py:352
  68.6 4.0 %collective-permute-start.3 = (f32[16,40,128]{2,1,0:T(8,128)S(1)}, f32[16,40,128]{2,1,0:T(8,128)S(1)}, u32[]{:S(2)}, u32[]{:S(2)}) collective-permute-start(f32[16,40,128]{2,1,0:T(8,128)S(1)} %all_to_all.17.refs_0_), channel_id=1, source_target_pairs={{0,8},{8,0},{1,9},{9,1},{2,10},{10,2},{3,11},{11,3},{4,12},{12,4},... | collective-permute-start | bytes 983048 | tf_op jit(solution)/shard_map/ppermute | solution.py:314
  72.6 1.3 %collective-permute-done.3.refs_1_ = f32[16,40,128]{2,1,0:T(8,128)S(1)} collective-permute-done((f32[16,40,128]{2,1,0:T(8,128)S(1)}, f32[16,40,128]{2,1,0:T(8,128)S(1)}, u32[]{:S(2)}, u32[]{:S(2)}) %collective-permute-start.3) | collective-permute-done | bytes 327712 | tf_op jit(solution)/shard_map/ppermute | solution.py:314
  73.9 0.9 %unpack.1 = (f32[512,128]{1,0:T(8,128)}, f32[512,128]{1,0:T(8,128)}, f32[1,512]{1,0:T(1,128)}) custom-call(s32[1]{0:T(128)} %bitcast.7.at_ref, f32[16,40,128]{2,1,0:T(8,128)S(1)} %all_to_all.17.refs_0_, f32[16,40,128]{2,1,0:T(8,128)S(1)} %collective-permute-done.3.refs_1_), custom_call_target="tpu_custom_call" | custom-call | tf_op jit(solution)/shard_map/unpack/pallas_call | solution.py:355
  (2 shorter events, 0.0 us)
Async XLA Ops:
  28.3 4.9 %collective-permute-start = (f32[8,40,128]{2,1,0:T(8,128)S(1)}, f32[8,40,128]{2,1,0:T(8,128)S(1)}, u32[]{:S(2)}, u32[]{:S(2)}) collective-permute-start(f32[8,40,128]{2,1,0:T(8,128)S(1)} %get-tuple-element.25), channel_id=1, source_target_pairs={{0,8},{8,0},{1,9},{9,1},{2,10},{10,2},{3,11},{11,3},{4,12},{12,4},... | collective-permute-start | bytes 491528 | tf_op jit(solution)/shard_map/ppermute | solution.py:314
  35.7 3.0 %collective-permute-start.1 = (f32[8,40,128]{2,1,0:T(8,128)S(1)}, f32[8,40,128]{2,1,0:T(8,128)S(1)}, u32[]{:S(2)}, u32[]{:S(2)}) collective-permute-start(f32[8,40,128]{2,1,0:T(8,128)S(1)} %moment.7), channel_id=1, source_target_pairs={{0,8},{8,0},{1,9},{9,1},{2,10},{10,2},{3,11},{11,3},{4,12},{12,4},... | collective-permute-start | bytes 491528 | tf_op jit(solution)/shard_map/ppermute | solution.py:314
  35.8 5.4 %collective-permute-start.2 = (f32[8,40,128]{2,1,0:T(8,128)S(1)}, f32[8,40,128]{2,1,0:T(8,128)S(1)}, u32[]{:S(2)}, u32[]{:S(2)}) collective-permute-start(f32[8,40,128]{2,1,0:T(8,128)S(1)} %add.23), channel_id=1, source_target_pairs={{0,16},{16,0},{1,17},{17,1},{2,18},{18,2},{3,19},{19,3},{4,20},{20... | collective-permute-start | bytes 491528 | tf_op jit(solution)/shard_map/ppermute | solution.py:314
  68.6 5.3 %collective-permute-start.3 = (f32[16,40,128]{2,1,0:T(8,128)S(1)}, f32[16,40,128]{2,1,0:T(8,128)S(1)}, u32[]{:S(2)}, u32[]{:S(2)}) collective-permute-start(f32[16,40,128]{2,1,0:T(8,128)S(1)} %all_to_all.17.refs_0_), channel_id=1, source_target_pairs={{0,8},{8,0},{1,9},{9,1},{2,10},{10,2},{3,11},{11,3},{4,12},{12,4},... | collective-permute-start | bytes 983048 | tf_op jit(solution)/shard_map/ppermute | solution.py:314
where the time goes:
time: 75 us; the launch traced here: 74.8 us
  blocking collectives  42.1 us (56%)
  Pallas kernels  21.3 us (28%)
  starting transfers between devices  6.88 us (9%)
  waiting for transfers between devices  3.76 us (5%)
    all_to_all x1, blocking collectives, per_device(): parts = lax.all_to_all(summed(mine, other, away), 'z', 0, 0, tiled=True)  16.4 us
    all_to_all x1, blocking collectives, per_device(): everyone = lax.all_to_all(local, COMP, 0, 0, tiled=True)  14.9 us
    all_to_all x1, blocking collectives, per_device(): near = lax.all_to_all(part, RING, 0, 0, tiled=True)  10.8 us
    pallas_call x4, Pallas kernels, moments(): pl.pallas_call(kernel, grid_spec=pltpu.PrefetchScalarGridSpec(num_scalar_...  10.7 us
    pallas_call x1, Pallas kernels, densities(): pl.pallas_call(density_kernel, in_specs=[smem] + [hbm] * 4, out_specs=[vm...  9.46 us
    ppermute x4, starting transfers between devices, exchanged(): return lax.ppermute(array, axis, [(0, 1), (1, 0)])  6.88 us
    ppermute x4, waiting for transfers between devices, exchanged(): return lax.ppermute(array, axis, [(0, 1), (1, 0)])  3.76 us
  transfers between devices with their start and end apart: 4, of which 2 were waited for; matrix products, arithmetic and copies ran while one was open for 0% of the time, Pallas kernels for 7%

commit v1 on v0

--- a/solution.py
+++ b/solution.py
@@ -160,8 +160,7 @@
 
 def moment_kernel(table_ref, e_ref, p_ref, q_ref, m_ref, sum_ref, *refs, block, first, places):
     if first:
-        lik_hbm, total_ref, *refs = refs
-        *refs, lik_ref, sem = refs
+        lik_ref, total_ref, *refs = refs
     else:
         total_ref = sum_ref
     *out_refs, acc_ref, cnt_ref = refs
@@ -180,7 +179,6 @@
             total = top + jnp.log2(jnp.sum(jnp.exp2(sums - top[None]), axis=0))
             total_ref[...] = total
             lik_ref[...] = total * LN2
-            pltpu.make_async_copy(lik_ref, lik_hbm, sem).start()
 
     def mul(a, b):
         return jnp.dot(a, b, preferred_element_type=F32)
@@ -213,8 +211,6 @@
 
     @pl.when(step == pl.num_programs(0) - 1)
     def _():
-        if first:
-            pltpu.make_async_copy(lik_ref, lik_hbm, sem).wait()
         count = jnp.sum(cnt_ref[...], axis=1, keepdims=True)
         count = jnp.broadcast_to(count, cnt_ref.shape).reshape(-1, pieces, 2, ROWS // 2, d)
         lane = lax.broadcasted_iota(jnp.int32, (pieces, ROWS // 2, d), 2)
@@ -239,9 +235,8 @@
     out_shape = [pltpu.VMEM((pieces, TALL, d), F32) for _ in places]
     scratch = [pltpu.VMEM((rows, 2 * d), F32), pltpu.VMEM((rows, 128), F32)]
     if first:
-        out_specs = [pl.BlockSpec(memory_space=pltpu.HBM), vmem, *out_specs]
-        out_shape = [pltpu.HBM((n // 128, 128), F32), pltpu.VMEM((n // 128, 128), F32), *out_shape]
-        scratch += [pltpu.VMEM((n // 128, 128), F32), pltpu.SemaphoreType.DMA]
+        out_specs = [vmem, vmem, *out_specs]
+        out_shape = [pltpu.VMEM((n // 128, 128), F32)] * 2 + out_shape
     return pl.pallas_call(
         kernel,
         grid_spec=pltpu.PrefetchScalarGridSpec(

time: 75 us -> 74.4 us (level)
  transfers between devices with their start and end apart: 4 -> 4, of which waited for: 2 -> 2; matrix products, arithmetic and copies ran while one was open for 0% -> 1% of each run, Pallas kernels for 7% -> 7%
where the time goes in v1:
time: 74.4 us; the launch traced here: 74.2 us
  blocking collectives  42.1 us (57%)
  Pallas kernels  20.7 us (28%)
  starting transfers between devices  6.88 us (9%)
  waiting for transfers between devices  3.14 us (4%)
    all_to_all x1, blocking collectives, per_device(): parts = lax.all_to_all(summed(mine, other, away), 'z', 0, 0, tiled=True)  16.4 us
    all_to_all x1, blocking collectives, per_device(): everyone = lax.all_to_all(local, COMP, 0, 0, tiled=True)  14.9 us
    all_to_all x1, blocking collectives, per_device(): near = lax.all_to_all(part, RING, 0, 0, tiled=True)  10.8 us
    pallas_call x4, Pallas kernels, moments(): pl.pallas_call(kernel, grid_spec=pltpu.PrefetchScalarGridSpec(num_scalar_...  10.1 us
    pallas_call x1, Pallas kernels, densities(): pl.pallas_call(density_kernel, in_specs=[smem] + [hbm] * 4, out_specs=[vm...  9.46 us
    ppermute x4, starting transfers between devices, exchanged(): return lax.ppermute(array, axis, [(0, 1), (1, 0)])  6.88 us
    ppermute x4, waiting for transfers between devices, exchanged(): return lax.ppermute(array, axis, [(0, 1), (1, 0)])  3.14 us
  transfers between devices with their start and end apart: 4, of which 2 were waited for; matrix products, arithmetic and copies ran while one was open for 1% of the time, Pallas kernels for 7%

profile of v1, /device:TPU:1, one launch (start us, length us, event | category | flops | bytes accessed | tf_op | source)
XLA Modules:
  0.0 74.2 jit_solution(3262457585632481470)
XLA Ops:
  0.6 0.1 stack.23.table_ref.refs_0_
  0.7 9.5 %density.1 = (f32[32,512,256]{2,1,0:T(8,128)S(1)}, bf16[8192,256]{1,0:T(8,128)(2,1)S(1)}, bf16[8192,256]{1,0:T(8,128)(2,1)S(1)}, f32[128,8192]{1,0:T(8,128)S(1)}...) custom-call(s32[5]{0:T(128)S(1)} %stack.23.table_ref.refs_0_, f32[8192,128]{1,0:T(8,128)} %x_hbm.1, ...), custom_call_target="tpu_custom_call" | custom-call | flops 6442450944 | bytes 20971520 | tf_op jit(solution)/shard_map/density/pallas_call | solution.py:117
  10.2 14.9 %all_to_all.15.refs_5_ = f32[8,64,128]{2,1,0:T(8,128)S(1)} all-to-all(f32[8,64,128]{2,1,0:T(8,128)S(1)} %get-tuple-element.22), channel_id=1, replica_groups=mesh['z'=8,'xl'=2,'co'=2,'y'=4,'xh'=2] {'y','xh'}, dimensions={0} | all-to-all | bytes 524288 | tf_op jit(solution)/shard_map/all_to_all | solution.py:326
  25.1 2.6 %moment.4 = (f32[64,128]{1,0:T(8,128)S(1)}, f32[64,128]{1,0:T(8,128)S(1)}, f32[8,40,128]{2,1,0:T(8,128)S(1)}) custom-call(s32[5]{0:T(128)S(1)} %stack.23.table_ref.refs_0_, f32[32,512,256]{2,1,0:T(8,128)S(1)} %get-tuple-element.18.refs_1_, bf16[8192,256]{1,0:T(8,128)(2,1)S(1)} %get-tuple-element.19.refs_2_, bf16[8192,256]{1,0:T(8,128)(2,1)S(1)} %get-tuple-element.20.refs_3_, ...), custom_call_target="tpu_custom_call" | custom-call | flops 1610612736 | bytes 8388608 | tf_op jit(solution)/shard_map/moment/pallas_call | solution.py:240
  27.7 2.4 %collective-permute-start = (f32[8,40,128]{2,1,0:T(8,128)S(1)}, f32[8,40,128]{2,1,0:T(8,128)S(1)}, u32[]{:S(2)}, u32[]{:S(2)}) collective-permute-start(f32[8,40,128]{2,1,0:T(8,128)S(1)} %get-tuple-element.25), channel_id=1, source_target_pairs={{0,8},{8,0},{1,9},{9,1},{2,10},{10,2},{3,11},{11,3},{4,12},{12,4},... | collective-permute-start | bytes 491528 | tf_op jit(solution)/shard_map/ppermute | solution.py:309
  30.0 2.5 %moment.5.refs_0_ = f32[8,40,128]{2,1,0:T(8,128)S(1)} custom-call(s32[5]{0:T(128)S(1)} %stack.23.table_ref.refs_0_, f32[32,512,256]{2,1,0:T(8,128)S(1)} %get-tuple-element.18.refs_1_, bf16[8192,256]{1,0:T(8,128)(2,1)S(1)} %get-tuple-element.19.refs_2_, bf16[8192,256]{1,0:T(8,128)(2,1)S(1)} %get-tuple-element.20.refs_3_, ...), custom_call_target="tpu_custom_call" | custom-call | flops 1610612736 | bytes 8388608 | tf_op jit(solution)/shard_map/moment/pallas_call | solution.py:240
  32.6 0.0 collective-permute-done.refs_1_
  32.6 2.5 %moment.7 = f32[8,40,128]{2,1,0:T(8,128)S(1)} custom-call(s32[5]{0:T(128)S(1)} %stack.23.table_ref.refs_0_, f32[32,512,256]{2,1,0:T(8,128)S(1)} %get-tuple-element.18.refs_1_, bf16[8192,256]{1,0:T(8,128)(2,1)S(1)} %get-tuple-element.19.refs_2_, bf16[8192,256]{1,0:T(8,128)(2,1)S(1)} %get-tuple-element.20.refs_3_, f32[128,8192]{1,0:T(8,128)S(1)} %get-tuple-element.21.refs_4_, ...), custom_call_target="tpu_custom_call" | custom-call | flops 1610612736 | bytes 8388608 | tf_op jit(solution)/shard_map/moment/pallas_call | solution.py:240
  35.1 0.1 collective-permute-start.1
  35.2 0.4 collective-permute-start.2
  35.6 2.5 %moment.6.refs_0_ = f32[8,40,128]{2,1,0:T(8,128)S(1)} custom-call(s32[5]{0:T(128)S(1)} %stack.23.table_ref.refs_0_, f32[32,512,256]{2,1,0:T(8,128)S(1)} %get-tuple-element.18.refs_1_, bf16[8192,256]{1,0:T(8,128)(2,1)S(1)} %get-tuple-element.19.refs_2_, bf16[8192,256]{1,0:T(8,128)(2,1)S(1)} %get-tuple-element.20.refs_3_, ...), custom_call_target="tpu_custom_call" | custom-call | flops 1610612736 | bytes 8388608 | tf_op jit(solution)/shard_map/moment/pallas_call | solution.py:240
  38.2 0.0 collective-permute-done.1.refs_1_
  38.2 2.5 %collective-permute-done.2.refs_2_ = f32[8,40,128]{2,1,0:T(8,128)S(1)} collective-permute-done((f32[8,40,128]{2,1,0:T(8,128)S(1)}, f32[8,40,128]{2,1,0:T(8,128)S(1)}, u32[]{:S(2)}, u32[]{:S(2)}) %collective-permute-start.2) | collective-permute-done | bytes 163872 | tf_op jit(solution)/shard_map/ppermute | solution.py:309
  40.7 16.4 %all_to_all.16.refs_0_ = f32[8,40,128]{2,1,0:T(8,128)S(1)} all-to-all(f32[8,40,128]{2,1,0:T(8,128)S(1)} %add.24), channel_id=1, replica_groups=mesh['z'=8,'xl'=2,'co'=2,'y'=4,'xh'=2] {'z'}, dimensions={0} | all-to-all | bytes 327680 | tf_op jit(solution)/shard_map/all_to_all | solution.py:339
  57.1 0.2 update.1
  57.2 10.8 %all_to_all.17.refs_0_ = f32[16,40,128]{2,1,0:T(8,128)S(1)} all-to-all(f32[16,40,128]{2,1,0:T(8,128)S(1)} %update.1), channel_id=1, replica_groups=mesh['z'=8,'xl'=2,'co'=2,'y'=4,'xh'=2] {'xl','z'}, dimensions={0} | all-to-all | bytes 655360 | tf_op jit(solution)/shard_map/all_to_all | solution.py:347
  68.0 4.0 %collective-permute-start.3 = (f32[16,40,128]{2,1,0:T(8,128)S(1)}, f32[16,40,128]{2,1,0:T(8,128)S(1)}, u32[]{:S(2)}, u32[]{:S(2)}) collective-permute-start(f32[16,40,128]{2,1,0:T(8,128)S(1)} %all_to_all.17.refs_0_), channel_id=1, source_target_pairs={{0,8},{8,0},{1,9},{9,1},{2,10},{10,2},{3,11},{11,3},{4,12},{12,4},... | collective-permute-start | bytes 983048 | tf_op jit(solution)/shard_map/ppermute | solution.py:309
  72.0 0.6 copy.8
  72.6 0.6 collective-permute-done.3.refs_1_
  73.3 0.9 %unpack.1 = (f32[512,128]{1,0:T(8,128)}, f32[512,128]{1,0:T(8,128)}, f32[1,512]{1,0:T(1,128)}) custom-call(s32[1]{0:T(128)} %bitcast.7.at_ref, f32[16,40,128]{2,1,0:T(8,128)S(1)} %all_to_all.17.refs_0_, f32[16,40,128]{2,1,0:T(8,128)S(1)} %collective-permute-done.3.refs_1_), custom_call_target="tpu_custom_call" | custom-call | tf_op jit(solution)/shard_map/unpack/pallas_call | solution.py:350
  (2 shorter events, 0.0 us)
Async XLA Ops:
  27.7 4.9 %collective-permute-start = (f32[8,40,128]{2,1,0:T(8,128)S(1)}, f32[8,40,128]{2,1,0:T(8,128)S(1)}, u32[]{:S(2)}, u32[]{:S(2)}) collective-permute-start(f32[8,40,128]{2,1,0:T(8,128)S(1)} %get-tuple-element.25), channel_id=1, source_target_pairs={{0,8},{8,0},{1,9},{9,1},{2,10},{10,2},{3,11},{11,3},{4,12},{12,4},... | collective-permute-start | bytes 491528 | tf_op jit(solution)/shard_map/ppermute | solution.py:309
  35.1 3.0 %collective-permute-start.1 = (f32[8,40,128]{2,1,0:T(8,128)S(1)}, f32[8,40,128]{2,1,0:T(8,128)S(1)}, u32[]{:S(2)}, u32[]{:S(2)}) collective-permute-start(f32[8,40,128]{2,1,0:T(8,128)S(1)} %moment.7), channel_id=1, source_target_pairs={{0,8},{8,0},{1,9},{9,1},{2,10},{10,2},{3,11},{11,3},{4,12},{12,4},... | collective-permute-start | bytes 491528 | tf_op jit(solution)/shard_map/ppermute | solution.py:309
  35.2 5.4 %collective-permute-start.2 = (f32[8,40,128]{2,1,0:T(8,128)S(1)}, f32[8,40,128]{2,1,0:T(8,128)S(1)}, u32[]{:S(2)}, u32[]{:S(2)}) collective-permute-start(f32[8,40,128]{2,1,0:T(8,128)S(1)} %add.23), channel_id=1, source_target_pairs={{0,16},{16,0},{1,17},{17,1},{2,18},{18,2},{3,19},{19,3},{4,20},{20... | collective-permute-start | bytes 491528 | tf_op jit(solution)/shard_map/ppermute | solution.py:309
  68.0 5.3 %collective-permute-start.3 = (f32[16,40,128]{2,1,0:T(8,128)S(1)}, f32[16,40,128]{2,1,0:T(8,128)S(1)}, u32[]{:S(2)}, u32[]{:S(2)}) collective-permute-start(f32[16,40,128]{2,1,0:T(8,128)S(1)} %all_to_all.17.refs_0_), channel_id=1, source_target_pairs={{0,8},{8,0},{1,9},{9,1},{2,10},{10,2},{3,11},{11,3},{4,12},{12,4},... | collective-permute-start | bytes 983048 | tf_op jit(solution)/shard_map/ppermute | solution.py:309

commit v2 on v1

--- a/solution.py
+++ b/solution.py
@@ -169,16 +169,12 @@
     pieces, _, d = out_refs[0].shape
     groups = pieces * ROWS // size
 
-    @pl.when(step == 0)
-    def _():
-        acc_ref[...] = jnp.zeros_like(acc_ref)
-        cnt_ref[...] = jnp.zeros_like(cnt_ref)
-        if first:
-            sums = sum_ref[...]
-            top = jnp.max(sums, axis=0)
-            total = top + jnp.log2(jnp.sum(jnp.exp2(sums - top[None]), axis=0))
-            total_ref[...] = total
-            lik_ref[...] = total * LN2
+    if first:
+        sums = sum_ref[...]
+        top = jnp.max(sums, axis=0)
+        total = top + jnp.log2(jnp.sum(jnp.exp2(sums - top[None]), axis=0))
+        total_ref[...] = total
+        lik_ref[...] = total * LN2
 
     def mul(a, b):
         return jnp.dot(a, b, preferred_element_type=F32)
@@ -206,8 +202,8 @@
         ph = p_ref[some, :]
         part = mul(rh, ph) + mul(rl, ph) + mul(rh, q_ref[some, :])
         acc = part if tile == 0 else acc + part
-    cnt_ref[...] += count
-    acc_ref[...] += acc
+    cnt_ref[...] = count
+    acc_ref[...] = acc
 
     @pl.when(step == pl.num_programs(0) - 1)
     def _():
@@ -286,14 +282,22 @@
         out_ref[i, 2 * ROWS :, :] = logw
 
 
-def unpack_kernel(at_ref, *refs):
-    *parts, mean_ref, var_ref, logw_ref = refs
-    d = mean_ref.shape[1]
-    rows = mean_ref.shape[0] // len(parts)
-    for i, ref in enumerate(parts):
-        at = pl.ds(pl.multiple_of((at_ref[0] if i == 0 else 1 - at_ref[0]) * rows, rows), rows)
-        mean_ref[at, :] = ref[:, :ROWS, :].reshape(rows, d)
-        var_ref[at, :] = ref[:, ROWS : 2 * ROWS, :].reshape(rows, d)
+def unpack_kernel(core_ref, near_ref, far_ref, mean_hbm, var_hbm, logw_hbm, row_ref, sems):
+    pieces, _, d = near_ref.shape
+    rows = pieces * ROWS
+    halves_of = ((core_ref[0], near_ref), (1 - core_ref[0], far_ref))
+    copies = []
+    for i, (half, ref) in enumerate(halves_of):
+        some = pl.ds(pl.multiple_of(half * pieces, pieces), pieces)
+        copies += [
+            pltpu.make_async_copy(ref.at[:, :ROWS, :], mean_hbm.at[some, :, :], sems.at[2 * i]),
+            pltpu.make_async_copy(
+                ref.at[:, ROWS : 2 * ROWS, :], var_hbm.at[some, :, :], sems.at[2 * i + 1]
+            ),
+        ]
+    for copy in copies:
+        copy.start()
+    for half, ref in halves_of:
         pair = ref[:, 2 * ROWS :, :]
         both = jnp.concatenate(
             [
@@ -302,7 +306,29 @@
             ],
             axis=1,
         ).reshape(rows, d)
-        logw_ref[:, at] = jnp.swapaxes(both, 0, 1)[:1, :]
+        row_ref[:, pl.ds(pl.multiple_of(half * rows, rows), rows)] = jnp.swapaxes(both, 0, 1)[:1, :]
+    copies.append(pltpu.make_async_copy(row_ref, logw_hbm, sems.at[4]))
+    copies[-1].start()
+    for copy in copies:
+        copy.wait()
+
+
+def unpacked(core, near, far):
+    pieces, _, d = near.shape
+    smem, vmem, hbm = (pl.BlockSpec(memory_space=s) for s in (pltpu.SMEM, pltpu.VMEM, pltpu.HBM))
+    return pl.pallas_call(
+        unpack_kernel,
+        in_specs=[smem, vmem, vmem],
+        out_specs=[hbm] * 3,
+        out_shape=[
+            pltpu.HBM((2 * pieces, ROWS, d), F32),
+            pltpu.HBM((2 * pieces, ROWS, d), F32),
+            pltpu.HBM((1, 2 * pieces * ROWS), F32),
+        ],
+        scratch_shapes=[pltpu.VMEM((1, 2 * pieces * ROWS), F32), pltpu.SemaphoreType.DMA((5,))],
+        compiler_params=pltpu.CompilerParams(vmem_limit_bytes=4 << 20),
+        name="unpack",
+    )(core.reshape(1), *in_vmem(near, far))
 
 
 def exchanged(array, axis):
@@ -345,19 +371,9 @@
         update, out_shape=pltpu.VMEM((ring, TALL, d), F32), name="update"
     )(*in_vmem(parts, own))
     near = lax.all_to_all(part, RING, 0, 0, tiled=True)
-    fresh = [near, exchanged(near, "co")]
-    smem, vmem = (pl.BlockSpec(memory_space=s) for s in (pltpu.SMEM, pltpu.VMEM))
-    fresh_means, fresh_vars, fresh_logw = pl.pallas_call(
-        unpack_kernel,
-        in_specs=[smem] + [vmem] * 2,
-        out_shape=[
-            jax.ShapeDtypeStruct((k, d), F32),
-            jax.ShapeDtypeStruct((k, d), F32),
-            jax.ShapeDtypeStruct((1, k), F32),
-        ],
-        name="unpack",
-    )(core.reshape(1), *in_vmem(*fresh))
-    return (lik.reshape(n), fresh_means, fresh_vars, fresh_logw.reshape(k))
+    far = exchanged(near, "co")
+    fresh_means, fresh_vars, fresh_logw = unpacked(core, near, far)
+    return (lik.reshape(n), fresh_means.reshape(k, d), fresh_vars.reshape(k, d), fresh_logw.reshape(k))
 
 
 def solution(mesh):

time: 74.4 us -> 74.5 us (level)
  no operation moved by 1% of the time
where the time goes in v2:
time: 74.5 us; the launch traced here: 74.3 us
  blocking collectives  42.1 us (57%)
  Pallas kernels  20.6 us (28%)
  starting transfers between devices  6.88 us (9%)
  waiting for transfers between devices  3.14 us (4%)
  between operations  0.88 us (1%)
    all_to_all x1, blocking collectives, per_device(): parts = lax.all_to_all(summed(mine, other, away), 'z', 0, 0, tiled=True)  16.4 us
    all_to_all x1, blocking collectives, per_device(): everyone = lax.all_to_all(local, COMP, 0, 0, tiled=True)  14.9 us
    all_to_all x1, blocking collectives, per_device(): near = lax.all_to_all(part, RING, 0, 0, tiled=True)  10.8 us
    pallas_call x4, Pallas kernels, moments(): pl.pallas_call(kernel, grid_spec=pltpu.PrefetchScalarGridSpec(num_scalar_...  10.1 us
    pallas_call x1, Pallas kernels, densities(): pl.pallas_call(density_kernel, in_specs=[smem] + [hbm] * 4, out_specs=[vm...  9.46 us
    ppermute x4, starting transfers between devices, exchanged(): return lax.ppermute(array, axis, [(0, 1), (1, 0)])  6.88 us
    ppermute x4, waiting for transfers between devices, exchanged(): return lax.ppermute(array, axis, [(0, 1), (1, 0)])  3.14 us
  transfers between devices with their start and end apart: 4, of which 2 were waited for; matrix products, arithmetic and copies ran while one was open for 1% of the time, Pallas kernels for 7%

profile of v2, /device:TPU:1, one launch (start us, length us, event | category | flops | bytes accessed | tf_op | source)
XLA Modules:
  0.0 74.3 jit_solution(9062774287889554761)
XLA Ops:
  0.6 0.1 stack.23.table_ref.refs_0_
  0.7 9.5 %density.1 = (f32[32,512,256]{2,1,0:T(8,128)S(1)}, bf16[8192,256]{1,0:T(8,128)(2,1)S(1)}, bf16[8192,256]{1,0:T(8,128)(2,1)S(1)}, f32[128,8192]{1,0:T(8,128)S(1)}...) custom-call(s32[5]{0:T(128)S(1)} %stack.23.table_ref.refs_0_, f32[8192,128]{1,0:T(8,128)} %x_hbm.1, ...), custom_call_target="tpu_custom_call" | custom-call | flops 6442450944 | bytes 20971520 | tf_op jit(solution)/shard_map/density/pallas_call | solution.py:117
  10.2 14.9 %all_to_all.15.refs_5_ = f32[8,64,128]{2,1,0:T(8,128)S(1)} all-to-all(f32[8,64,128]{2,1,0:T(8,128)S(1)} %get-tuple-element.22), channel_id=1, replica_groups=mesh['z'=8,'xl'=2,'co'=2,'y'=4,'xh'=2] {'y','xh'}, dimensions={0} | all-to-all | bytes 524288 | tf_op jit(solution)/shard_map/all_to_all | solution.py:352
  25.1 2.6 %moment.4 = (f32[64,128]{1,0:T(8,128)S(1)}, f32[64,128]{1,0:T(8,128)S(1)}, f32[8,40,128]{2,1,0:T(8,128)S(1)}) custom-call(s32[5]{0:T(128)S(1)} %stack.23.table_ref.refs_0_, f32[32,512,256]{2,1,0:T(8,128)S(1)} %get-tuple-element.18.refs_1_, bf16[8192,256]{1,0:T(8,128)(2,1)S(1)} %get-tuple-element.19.refs_2_, bf16[8192,256]{1,0:T(8,128)(2,1)S(1)} %get-tuple-element.20.refs_3_, ...), custom_call_target="tpu_custom_call" | custom-call | flops 1610612736 | bytes 8388608 | tf_op jit(solution)/shard_map/moment/pallas_call | solution.py:236
  27.7 2.4 %collective-permute-start = (f32[8,40,128]{2,1,0:T(8,128)S(1)}, f32[8,40,128]{2,1,0:T(8,128)S(1)}, u32[]{:S(2)}, u32[]{:S(2)}) collective-permute-start(f32[8,40,128]{2,1,0:T(8,128)S(1)} %get-tuple-element.25), channel_id=1, source_target_pairs={{0,8},{8,0},{1,9},{9,1},{2,10},{10,2},{3,11},{11,3},{4,12},{12,4},... | collective-permute-start | bytes 491528 | tf_op jit(solution)/shard_map/ppermute | solution.py:335
  30.0 2.5 %moment.5.refs_0_ = f32[8,40,128]{2,1,0:T(8,128)S(1)} custom-call(s32[5]{0:T(128)S(1)} %stack.23.table_ref.refs_0_, f32[32,512,256]{2,1,0:T(8,128)S(1)} %get-tuple-element.18.refs_1_, bf16[8192,256]{1,0:T(8,128)(2,1)S(1)} %get-tuple-element.19.refs_2_, bf16[8192,256]{1,0:T(8,128)(2,1)S(1)} %get-tuple-element.20.refs_3_, ...), custom_call_target="tpu_custom_call" | custom-call | flops 1610612736 | bytes 8388608 | tf_op jit(solution)/shard_map/moment/pallas_call | solution.py:236
  32.6 0.0 collective-permute-done.refs_1_
  32.6 2.5 %moment.7 = f32[8,40,128]{2,1,0:T(8,128)S(1)} custom-call(s32[5]{0:T(128)S(1)} %stack.23.table_ref.refs_0_, f32[32,512,256]{2,1,0:T(8,128)S(1)} %get-tuple-element.18.refs_1_, bf16[8192,256]{1,0:T(8,128)(2,1)S(1)} %get-tuple-element.19.refs_2_, bf16[8192,256]{1,0:T(8,128)(2,1)S(1)} %get-tuple-element.20.refs_3_, f32[128,8192]{1,0:T(8,128)S(1)} %get-tuple-element.21.refs_4_, ...), custom_call_target="tpu_custom_call" | custom-call | flops 1610612736 | bytes 8388608 | tf_op jit(solution)/shard_map/moment/pallas_call | solution.py:236
  35.1 0.1 collective-permute-start.1
  35.2 0.4 collective-permute-start.2
  35.6 2.5 %moment.6.refs_0_ = f32[8,40,128]{2,1,0:T(8,128)S(1)} custom-call(s32[5]{0:T(128)S(1)} %stack.23.table_ref.refs_0_, f32[32,512,256]{2,1,0:T(8,128)S(1)} %get-tuple-element.18.refs_1_, bf16[8192,256]{1,0:T(8,128)(2,1)S(1)} %get-tuple-element.19.refs_2_, bf16[8192,256]{1,0:T(8,128)(2,1)S(1)} %get-tuple-element.20.refs_3_, ...), custom_call_target="tpu_custom_call" | custom-call | flops 1610612736 | bytes 8388608 | tf_op jit(solution)/shard_map/moment/pallas_call | solution.py:236
  38.2 0.0 collective-permute-done.1.refs_1_
  38.2 2.5 %collective-permute-done.2.refs_2_ = f32[8,40,128]{2,1,0:T(8,128)S(1)} collective-permute-done((f32[8,40,128]{2,1,0:T(8,128)S(1)}, f32[8,40,128]{2,1,0:T(8,128)S(1)}, u32[]{:S(2)}, u32[]{:S(2)}) %collective-permute-start.2) | collective-permute-done | bytes 163872 | tf_op jit(solution)/shard_map/ppermute | solution.py:335
  40.7 16.4 %all_to_all.16.refs_0_ = f32[8,40,128]{2,1,0:T(8,128)S(1)} all-to-all(f32[8,40,128]{2,1,0:T(8,128)S(1)} %add.24), channel_id=1, replica_groups=mesh['z'=8,'xl'=2,'co'=2,'y'=4,'xh'=2] {'z'}, dimensions={0} | all-to-all | bytes 327680 | tf_op jit(solution)/shard_map/all_to_all | solution.py:365
  57.1 0.2 update.1
  57.2 10.8 %all_to_all.17.near_ref = f32[16,40,128]{2,1,0:T(8,128)S(1)} all-to-all(f32[16,40,128]{2,1,0:T(8,128)S(1)} %update.1), channel_id=1, replica_groups=mesh['z'=8,'xl'=2,'co'=2,'y'=4,'xh'=2] {'xl','z'}, dimensions={0} | all-to-all | bytes 655360 | tf_op jit(solution)/shard_map/all_to_all | solution.py:373
  68.0 4.0 %collective-permute-start.3 = (f32[16,40,128]{2,1,0:T(8,128)S(1)}, f32[16,40,128]{2,1,0:T(8,128)S(1)}, u32[]{:S(2)}, u32[]{:S(2)}) collective-permute-start(f32[16,40,128]{2,1,0:T(8,128)S(1)} %all_to_all.17.near_ref), channel_id=1, source_target_pairs={{0,8},{8,0},{1,9},{9,1},{2,10},{10,2},{3,11},{11,3},{4,12},{12,4},... | collective-permute-start | bytes 983048 | tf_op jit(solution)/shard_map/ppermute | solution.py:335
  72.0 0.6 copy.8
  72.6 0.6 collective-permute-done.3.far_ref
  73.3 0.8 %unpack.1 = (f32[32,16,128]{2,1,0:T(8,128)}, f32[32,16,128]{2,1,0:T(8,128)}, f32[1,512]{1,0:T(1,128)}) custom-call(s32[1]{0:T(128)} %bitcast.7.core_ref, f32[16,40,128]{2,1,0:T(8,128)S(1)} %all_to_all.17.near_ref, f32[16,40,128]{2,1,0:T(8,128)S(1)} %collective-permute-done.3.far_ref), custom_call_target="tpu_custom_call" | custom-call | tf_op jit(solution)/shard_map/unpack/pallas_call | solution.py:319
  (2 shorter events, 0.0 us)
Async XLA Ops:
  27.7 4.9 %collective-permute-start = (f32[8,40,128]{2,1,0:T(8,128)S(1)}, f32[8,40,128]{2,1,0:T(8,128)S(1)}, u32[]{:S(2)}, u32[]{:S(2)}) collective-permute-start(f32[8,40,128]{2,1,0:T(8,128)S(1)} %get-tuple-element.25), channel_id=1, source_target_pairs={{0,8},{8,0},{1,9},{9,1},{2,10},{10,2},{3,11},{11,3},{4,12},{12,4},... | collective-permute-start | bytes 491528 | tf_op jit(solution)/shard_map/ppermute | solution.py:335
  35.1 3.0 %collective-permute-start.1 = (f32[8,40,128]{2,1,0:T(8,128)S(1)}, f32[8,40,128]{2,1,0:T(8,128)S(1)}, u32[]{:S(2)}, u32[]{:S(2)}) collective-permute-start(f32[8,40,128]{2,1,0:T(8,128)S(1)} %moment.7), channel_id=1, source_target_pairs={{0,8},{8,0},{1,9},{9,1},{2,10},{10,2},{3,11},{11,3},{4,12},{12,4},... | collective-permute-start | bytes 491528 | tf_op jit(solution)/shard_map/ppermute | solution.py:335
  35.2 5.4 %collective-permute-start.2 = (f32[8,40,128]{2,1,0:T(8,128)S(1)}, f32[8,40,128]{2,1,0:T(8,128)S(1)}, u32[]{:S(2)}, u32[]{:S(2)}) collective-permute-start(f32[8,40,128]{2,1,0:T(8,128)S(1)} %add.23), channel_id=1, source_target_pairs={{0,16},{16,0},{1,17},{17,1},{2,18},{18,2},{3,19},{19,3},{4,20},{20... | collective-permute-start | bytes 491528 | tf_op jit(solution)/shard_map/ppermute | solution.py:335
  68.0 5.3 %collective-permute-start.3 = (f32[16,40,128]{2,1,0:T(8,128)S(1)}, f32[16,40,128]{2,1,0:T(8,128)S(1)}, u32[]{:S(2)}, u32[]{:S(2)}) collective-permute-start(f32[16,40,128]{2,1,0:T(8,128)S(1)} %all_to_all.17.near_ref), channel_id=1, source_target_pairs={{0,8},{8,0},{1,9},{9,1},{2,10},{10,2},{3,11},{11,3},{4,12},{12,4},... | collective-permute-start | bytes 983048 | tf_op jit(solution)/shard_map/ppermute | solution.py:335
